TPU v7x, 512 devices: a whole 4x8x8 slice. The times are simulated.
512 devices in a mesh: dp: 64 (over y, z), aug: 8 (over x, core).
Axes of the slice: x: 4, y: 8, z: 8, core: 2. Of those that a mesh axis runs over, the one named last changes fastest.
Arguments:
- images: bfloat16 [8, 64, 197, 768], P('aug', 'dp'), may hold values from -6 to 6
- out_grads: bfloat16 [8, 64, 197, 768], P('aug', 'dp'), may hold values from -8 to 8
- up_weight_t: bfloat16 [3072, 768], P(('dp', 'aug')), may hold values from -0.21875 to 0.21875
- down_weight_t: bfloat16 [3072, 768], P(('dp', 'aug')), may hold values from -0.21875 to 0.21875
- left_up: bfloat16 [3072, 128], P(('dp', 'aug')), may hold values from -0.109375 to 0.109375
- right_up: bfloat16 [768, 128], replicated, may hold values from -0.21875 to 0.21875
- left_down: bfloat16 [768, 128], replicated, may hold values from -0.21875 to 0.21875
- right_down: bfloat16 [3072, 128], P(('dp', 'aug')), may hold values from -0.109375 to 0.109375
- noise: float32 [2, 128, 128], P(None, 'aug'), may hold values from -6 to 6
Outputs:
- update: float32 [2, 128, 128], P(None, 'aug')
- clip_scales: float32 [64], P('dp')
All inputs are finite; a program needn't handle non-finite values.
Results may differ from a plain program's by a relative error of at most 0.0032.
Values may be sent and summed in bfloat16 or wider, within the bound.
No kernel may reach another device: no remote copies, remote signals or barrier semaphores. Data moves between devices by JAX's collectives and lax.ppermute only.
A program may use at most 64 MiB of HBM per device.

v0:
```python
import math
import jax
import jax.numpy as jnp
from jax import lax
from jax.sharding import Mesh
from jax.sharding import PartitionSpec as P

DP = ("dp_0", "dp_1")
DP_AUG = ("dp_0", "dp_1", "aug")
gelu_coef = 0.7978845608028654
clip_frac = 0.3
noise_mult = 0.05


def side_by_side(arrays, axis, dim, along):
    ends, at = ([], 0)
    for a in arrays[:-1]:
        at += a.shape[along]
        ends.append(at)
    both = jnp.concatenate(arrays, axis=along)
    return tuple(jnp.split(lax.all_gather(both, axis, axis=dim, tiled=True), ends, axis=along))


def copy_for_each(shard, axis):
    size = lax.axis_size(axis)
    return lax.all_to_all(
        jnp.broadcast_to(shard[None], (size, *shard.shape)), axis, 0, 0, tiled=True
    )


def of_everyone(shard, axis):
    return copy_for_each(shard, axis).sum(axis=0)


def by_axis(shard, axes):
    for axis in axes:
        shard = lax.psum(shard, axis)
    return shard


def gelu_pair(hidden):
    inner = gelu_coef * (hidden + 0.044715 * hidden * hidden * hidden)
    tangent = jnp.tanh(inner)
    value = 0.5 * hidden * (1.0 + tangent)
    slope = 0.5 * (1.0 + tangent) + 0.5 * hidden * (1.0 - tangent * tangent) * gelu_coef * (
        1.0 + 3.0 * 0.044715 * hidden * hidden
    )
    return (value, slope)


def contract_last(left, right):
    return lax.dot_general(
        left, right, (((1,), (1,)), ((), ())), preferred_element_type=jnp.float32
    )


def local(
    images, out_grads, up_weight_t, down_weight_t, left_up, right_up, left_down, right_down, noise
):
    local_augs = images.shape[0]
    local_images = images.shape[1]
    tokens = images.shape[2]
    width = images.shape[3]
    rank = right_up.shape[1]
    token_rows = images.reshape(-1, width)
    grad_rows = out_grads.reshape(-1, width)
    grouped = side_by_side((up_weight_t, down_weight_t, left_up, right_down), "aug", 0, 1)
    up_piece, down_piece, left_piece, right_piece = side_by_side(
        (grouped[0], grouped[1], grouped[2], grouped[3]), DP, 0, 1
    )
    hidden = contract_last(token_rows, up_piece)
    activation, slope = gelu_pair(hidden)
    back = contract_last(grad_rows, down_piece)
    hidden_grad = (back * slope).astype(jnp.bfloat16)
    first = jnp.dot(hidden_grad, left_piece, preferred_element_type=jnp.float32)
    second = jnp.dot(
        activation.astype(jnp.bfloat16), right_piece, preferred_element_type=jnp.float32
    )
    up_total = first
    down_total = second
    v_up = up_total.astype(jnp.bfloat16)
    u_down = down_total.astype(jnp.bfloat16)
    u_up = jnp.dot(token_rows, right_up, preferred_element_type=jnp.float32).astype(jnp.bfloat16)
    v_down = jnp.dot(grad_rows, left_down, preferred_element_type=jnp.float32).astype(jnp.bfloat16)
    shape = (local_augs, local_images, tokens, rank)
    first = jnp.einsum(
        "aitr,aits->irs",
        v_up.reshape(shape),
        u_up.reshape(shape),
        preferred_element_type=jnp.float32,
    )
    second = jnp.einsum(
        "aitr,aits->irs",
        v_down.reshape(shape),
        u_down.reshape(shape),
        preferred_element_type=jnp.float32,
    )
    local_terms = jnp.stack([first, second], axis=1)
    all_augs = local_augs * lax.axis_size("aug")
    share_rows = rank // lax.axis_size("aug")
    lower_row = lax.axis_index("aug") * share_rows
    summed_terms = of_everyone(local_terms, "aug")
    aug_mean = summed_terms / all_augs
    squares = jnp.sum(aug_mean * aug_mean, axis=(1, 2, 3))
    my_rows = lax.dynamic_slice_in_dim(aug_mean, lower_row, share_rows, 2)
    norms = jnp.sqrt(squares + 1e-06)
    clip_norm = clip_frac * rank * math.sqrt(tokens / all_augs)
    clip_scales = jnp.minimum(1.0, clip_norm / norms)
    clipped_rows = jnp.sum(clip_scales[:, None, None, None] * my_rows, axis=0)
    summed_rows = by_axis(clipped_rows, DP)
    all_images = local_images * lax.axis_size(DP)
    update = (summed_rows + noise_mult * clip_norm * noise) / jnp.sqrt(jnp.float32(all_images))
    return (update, clip_scales)


def solution(mesh):
    torus = Mesh(mesh.devices.reshape(8, 8, mesh.shape["aug"]), ("dp_0", "dp_1", "aug"))
    placed = (
        P("aug", DP, None, None),
        P("aug", DP, None, None),
        P(DP_AUG, None),
        P(DP_AUG, None),
        P(DP_AUG, None),
        P(),
        P(),
        P(DP_AUG, None),
        P(None, "aug", None),
    )
    return jax.shard_map(
        local, mesh=torus, in_specs=placed, out_specs=(P(None, "aug", None), P(DP)), check_vma=False
    )
```

profile of v0, /device:TPU:2, one launch (start us, length us, event | category | flops | bytes accessed | tf_op | source)
XLA Modules:
  0.0 238.5 jit_solution(18309758157067267480)
XLA Ops:
  7.2 0.0 copy-start
  7.2 0.0 all-gather.3.cloned.1.call-start
  7.2 0.8 maximum_bitcast_fusion.1
  8.0 15.5 %all-gather = bf16[8,6,1792]{2,1,0:T(8,128)(2,1)S(1)} all-gather(bf16[1,6,1792]{2,1,0:T(8,128)(2,1)S(1)} %maximum_bitcast_fusion.1), channel_id=1, replica_groups=mesh['dp_0'=8,'dp_1'=8,'aug'=8] {'aug'}, dimensions={0}, use_global_device_ids=true | all-gather | bytes 193536 | tf_op jit(solution)/shard_map/all_gather | solution.py:21
  23.5 0.7 reshape.63
  24.3 0.0 all-gather.3.cloned.1.call-update
  24.3 0.0 copy-start.1
  24.3 113.4 %all-gather.3.cloned.1.call-done = bf16[3072,1792]{1,0:T(8,128)(2,1)} async-done(((bf16[48,1792]{1,0:T(8,128)(2,1)}), bf16[3072,1792]{1,0:T(8,128)(2,1)}) %all-gather.3.cloned.1.call-update) | async-done | bytes 11010064 | tf_op jit(solution)/shard_map/all_gather | solution.py:21
  137.7 4.0 %fusion.7 = f32[197,3072]{1,0:T(8,128)S(1)} fusion(bf16[3072,1792]{1,0:T(8,128)(2,1)} %all-gather.3.cloned.1.call-done, bf16[1,1,197,768]{3,2,1,0:T(8,128)(2,1)S(1)} %copy-done), kind=kOutput, calls=%fused_computation.5 | convolution fusion | flops 929562624 | bytes 7441920 | tf_op jit(solution)/shard_map/dot_general | solution.py:52
  141.7 0.0 copy-start.2
  141.7 5.3 %fusion.30 = bf16[197,128]{1,0:T(8,128)(2,1)S(1)} fusion(bf16[3072,1792]{1,0:T(8,128)(2,1)} %all-gather.3.cloned.1.call-done, f32[197,3072]{1,0:T(8,128)S(1)} %fusion.7, bf16[1,1,197,768]{3,2,1,0:T(8,128)(2,1)S(1)} %copy-done.1), kind=kOutput, calls=%fused_computation.23 | convolution fusion | flops 1096013440 | bytes 8278784 | tf_op jit(solution)/shard_map/dot_general | solution.py:75
  147.0 0.4 convolution_bitcast_fusion.1
  147.4 0.0 copy-start.3
  147.4 2.2 fusion.33
  149.6 0.5 convolution_bitcast_fusion
  150.1 0.0 copy-start.4
  150.1 1.1 broadcast_in_dim.10
  151.2 4.8 %all-to-all-start = ((f32[8,1,2,128,128]{4,3,2,1,0:T(8,128)}), f32[8,1,2,128,128]{4,3,2,1,0:T(8,128)S(1)}, u32[]{:S(2)}, u32[]{:S(2)}) async-start(f32[8,1,2,128,128]{4,3,2,1,0:T(8,128)} %broadcast_in_dim.10), calls=%async_computation | async-start | bytes 2097152 | tf_op jit(solution)/shard_map/all_to_all | solution.py:26
  156.0 14.5 %all-to-all-done = f32[8,1,2,128,128]{4,3,2,1,0:T(8,128)S(1)} async-done(((f32[8,1,2,128,128]{4,3,2,1,0:T(8,128)}), f32[8,1,2,128,128]{4,3,2,1,0:T(8,128)S(1)}, u32[]{:S(2)}, u32[]{:S(2)}) %all-to-all-start) | async-done | bytes 1048608 | tf_op jit(solution)/shard_map/all_to_all | solution.py:26
  170.5 0.1 reduce_sum.16
  170.5 0.6 multiply_reduce_fusion
  171.9 29.7 %psum.14 = f32[2,16,128]{2,1,0:T(8,128)S(1)} all-reduce(f32[2,16,128]{2,1,0:T(8,128)S(1)} %dynamic-slice_multiply_fusion), channel_id=1, replica_groups=mesh['dp_0'=8,'dp_1'=8,'aug'=8] {'dp_0'}, use_global_device_ids=true, to_apply=%region_2.0 | all-reduce | flops 4096 | bytes 32768 | tf_op jit(solution)/shard_map/psum | solution.py:37
  201.6 28.3 %psum.15 = f32[2,16,128]{2,1,0:T(8,128)S(1)} all-reduce(f32[2,16,128]{2,1,0:T(8,128)S(1)} %psum.14), channel_id=1, replica_groups=mesh['dp_0'=8,'dp_1'=8,'aug'=8] {'dp_1'}, use_global_device_ids=true, to_apply=%region_3.0 | all-reduce | flops 4096 | bytes 32768 | tf_op jit(solution)/shard_map/psum | solution.py:37
  229.9 0.6 add_multiply_fusion
  (7 shorter events, 0.0 us)
Async XLA Ops:
  7.2 130.6 %copy-start = (bf16[1,1,197,768]{3,2,1,0:T(8,128)(2,1)S(1)}, bf16[1,1,197,768]{3,2,1,0:T(8,128)(2,1)}, u32[]{:S(2)}) copy-start(bf16[1,1,197,768]{3,2,1,0:T(8,128)(2,1)} %param.9) | copy-start | bytes 907780
  7.2 130.6 %all-gather.3.cloned.1.call-start = ((), (), s32[]{:S(2)}) async-start(), calls=%async_computation.1 | async-start | bytes 11182080 | tf_op jit(solution)/shard_map/all_gather | solution.py:21
  24.3 117.4 %copy-start.1 = (bf16[1,1,197,768]{3,2,1,0:T(8,128)(2,1)S(1)}, bf16[1,1,197,768]{3,2,1,0:T(8,128)(2,1)}, u32[]{:S(2)}) copy-start(bf16[1,1,197,768]{3,2,1,0:T(8,128)(2,1)} %param.10) | copy-start | bytes 907780
  141.7 5.3 %copy-start.2 = (bf16[768,128]{1,0:T(8,128)(2,1)S(1)}, bf16[768,128]{1,0:T(8,128)(2,1)}, u32[]{:S(2)}) copy-start(bf16[768,128]{1,0:T(8,128)(2,1)} %param.14) | copy-start | bytes 589828
  147.4 2.2 copy-start.3
  150.1 79.8 %copy-start.4 = (f32[2,16,128]{2,1,0:T(8,128)S(1)}, f32[2,16,128]{2,1,0:T(8,128)}, u32[]{:S(2)}) copy-start(f32[2,16,128]{2,1,0:T(8,128)} %param.17) | copy-start | bytes 49156
  151.2 19.3 %all-to-all-start = ((f32[8,1,2,128,128]{4,3,2,1,0:T(8,128)}), f32[8,1,2,128,128]{4,3,2,1,0:T(8,128)S(1)}, u32[]{:S(2)}, u32[]{:S(2)}) async-start(f32[8,1,2,128,128]{4,3,2,1,0:T(8,128)} %broadcast_in_dim.10), calls=%async_computation | async-start | bytes 2097152 | tf_op jit(solution)/shard_map/all_to_all | solution.py:26
Sparse Core Ops, SparseCore 0:
  24.4 113.2 all-gather.2
where the time goes:
time: 239 us
  waiting for transfers between devices  128 us (54%)
  blocking collectives  73.6 us (31%)
  between operations  16 us (7%)
  matrix products  12.2 us (5%)
  starting transfers between devices  4.83 us (2%)
    all_gather x1, waiting for transfers between devices, side_by_side(): lax.all_gather(both, axis, axis=dim, tiled=True)  113 us
    psum x2, blocking collectives, by_axis(): shard = lax.psum(shard, axis)  58.1 us
    all_gather x1, blocking collectives, side_by_side(): lax.all_gather(both, axis, axis=dim, tiled=True)  15.5 us
    all_to_all x1, waiting for transfers between devices, copy_for_each(): lax.all_to_all(jnp.broadcast_to(shard[None], (size, *shard.shape)), axis,...  14.5 us
    dot_general x1, matrix products, local(): first = jnp.dot(hidden_grad, left_piece, preferred_element_type=jnp.float32)  5.26 us
    all_to_all x1, starting transfers between devices, copy_for_each(): lax.all_to_all(jnp.broadcast_to(shard[None], (size, *shard.shape)), axis,...  4.79 us
  transfers between devices with their start and end apart: 2, of which 2 were waited for; matrix products, arithmetic and copies ran while one was open for 0% of the time, Pallas kernels for 0%

commit v1 on v0

--- a/solution.py
+++ b/solution.py
@@ -34,7 +34,7 @@
 
 def by_axis(shard, axes):
     for axis in axes:
-        shard = lax.psum(shard, axis)
+        shard = jnp.sum(lax.all_gather(shard, axis), axis=0)
     return shard
 
 

time: 239 us -> 232 us (0.971)
  the two profiles are of different devices: /device:TPU:2 before, /device:TPU:16 now
where the time goes in v1:
time: 232 us; the launch traced here: 231 us
  waiting for transfers between devices  132 us (57%)
  blocking collectives  63.3 us (27%)
  between operations  16 us (7%)
  matrix products  12.2 us (5%)
  starting transfers between devices  4.29 us (2%)
    all_gather x1, waiting for transfers between devices, side_by_side(): lax.all_gather(both, axis, axis=dim, tiled=True)  116 us
    all_gather x2, blocking collectives, by_axis(): shard = jnp.sum(lax.all_gather(shard, axis), axis=0)  50.1 us
    all_to_all x1, waiting for transfers between devices, copy_for_each(): lax.all_to_all(jnp.broadcast_to(shard[None], (size, *shard.shape)), axis,...  15.9 us
    all_gather x1, blocking collectives, side_by_side(): lax.all_gather(both, axis, axis=dim, tiled=True)  13.2 us
    dot_general x1, matrix products, local(): first = jnp.dot(hidden_grad, left_piece, preferred_element_type=jnp.float32)  5.26 us
  transfers between devices with their start and end apart: 2, of which 2 were waited for; matrix products, arithmetic and copies ran while one was open for 0% of the time, Pallas kernels for 0%

profile of v1, /device:TPU:16, one launch (start us, length us, event | category | flops | bytes accessed | tf_op | source)
XLA Modules:
  0.0 231.4 jit_solution(16102641114889778105)
XLA Ops:
  7.2 0.0 copy-start
  7.2 0.0 all-gather.5.cloned.1.call-start
  7.2 0.8 maximum_bitcast_fusion.1
  8.0 13.2 %all-gather.2 = bf16[8,6,1792]{2,1,0:T(8,128)(2,1)S(1)} all-gather(bf16[1,6,1792]{2,1,0:T(8,128)(2,1)S(1)} %maximum_bitcast_fusion.1), channel_id=1, replica_groups=mesh['dp_0'=8,'dp_1'=8,'aug'=8] {'aug'}, dimensions={0}, use_global_device_ids=true | all-gather | bytes 193536 | tf_op jit(solution)/shard_map/all_gather | solution.py:21
  21.2 0.7 reshape.65
  21.9 0.0 all-gather.5.cloned.1.call-update
  21.9 0.0 copy-start.1
  22.0 115.6 %all-gather.5.cloned.1.call-done = bf16[3072,1792]{1,0:T(8,128)(2,1)} async-done(((bf16[48,1792]{1,0:T(8,128)(2,1)}), bf16[3072,1792]{1,0:T(8,128)(2,1)}) %all-gather.5.cloned.1.call-update) | async-done | bytes 11010064 | tf_op jit(solution)/shard_map/all_gather | solution.py:21
  137.6 4.0 %fusion.7 = f32[197,3072]{1,0:T(8,128)S(1)} fusion(bf16[3072,1792]{1,0:T(8,128)(2,1)} %all-gather.5.cloned.1.call-done, bf16[1,1,197,768]{3,2,1,0:T(8,128)(2,1)S(1)} %copy-done), kind=kOutput, calls=%fused_computation.5 | convolution fusion | flops 929562624 | bytes 7441920 | tf_op jit(solution)/shard_map/dot_general | solution.py:52
  141.6 0.0 copy-start.2
  141.6 5.3 %fusion.30 = bf16[197,128]{1,0:T(8,128)(2,1)S(1)} fusion(bf16[3072,1792]{1,0:T(8,128)(2,1)} %all-gather.5.cloned.1.call-done, f32[197,3072]{1,0:T(8,128)S(1)} %fusion.7, bf16[1,1,197,768]{3,2,1,0:T(8,128)(2,1)S(1)} %copy-done.1), kind=kOutput, calls=%fused_computation.23 | convolution fusion | flops 1096013440 | bytes 8278784 | tf_op jit(solution)/shard_map/dot_general | solution.py:75
  146.9 0.4 convolution_bitcast_fusion.1
  147.3 0.0 copy-start.3
  147.3 2.2 fusion.33
  149.4 0.5 convolution_bitcast_fusion
  149.9 0.0 copy-start.4
  149.9 1.1 broadcast_in_dim.10
  151.0 4.3 %all-to-all-start = ((f32[8,1,2,128,128]{4,3,2,1,0:T(8,128)}), f32[8,1,2,128,128]{4,3,2,1,0:T(8,128)S(1)}, u32[]{:S(2)}, u32[]{:S(2)}) async-start(f32[8,1,2,128,128]{4,3,2,1,0:T(8,128)} %broadcast_in_dim.10), calls=%async_computation | async-start | bytes 2097152 | tf_op jit(solution)/shard_map/all_to_all | solution.py:26
  155.3 15.9 %all-to-all-done = f32[8,1,2,128,128]{4,3,2,1,0:T(8,128)S(1)} async-done(((f32[8,1,2,128,128]{4,3,2,1,0:T(8,128)}), f32[8,1,2,128,128]{4,3,2,1,0:T(8,128)S(1)}, u32[]{:S(2)}, u32[]{:S(2)}) %all-to-all-start) | async-done | bytes 1048608 | tf_op jit(solution)/shard_map/all_to_all | solution.py:26
  171.2 0.1 reduce_sum.40
  171.3 0.6 multiply_reduce_fusion
  172.6 25.5 %all-gather = f32[16,16,128]{2,1,0:T(8,128)S(1)} all-gather(f32[2,16,128]{2,1,0:T(8,128)S(1)} %dynamic-slice_multiply_fusion), channel_id=2, replica_groups=mesh['dp_0'=8,'dp_1'=8,'aug'=8] {'dp_0'}, dimensions={0}, use_global_device_ids=true | all-gather | bytes 147456 | tf_op jit(solution)/shard_map/all_gather | solution.py:37
  198.2 24.6 %all-gather.1 = f32[16,16,128]{2,1,0:T(8,128)S(1)} all-gather(f32[2,16,128]{2,1,0:T(8,128)S(1)} %reduce_sum.42), channel_id=3, replica_groups=mesh['dp_0'=8,'dp_1'=8,'aug'=8] {'dp_1'}, dimensions={0}, use_global_device_ids=true | all-gather | bytes 147456 | tf_op jit(solution)/shard_map/all_gather | solution.py:37
  222.8 0.6 add_multiply_fusion
  (9 shorter events, 0.1 us)
Async XLA Ops:
  7.2 130.4 %copy-start = (bf16[1,1,197,768]{3,2,1,0:T(8,128)(2,1)S(1)}, bf16[1,1,197,768]{3,2,1,0:T(8,128)(2,1)}, u32[]{:S(2)}) copy-start(bf16[1,1,197,768]{3,2,1,0:T(8,128)(2,1)} %param.9) | copy-start | bytes 907780
  7.2 130.4 %all-gather.5.cloned.1.call-start = ((), (), s32[]{:S(2)}) async-start(), calls=%async_computation.1 | async-start | bytes 11182080 | tf_op jit(solution)/shard_map/all_gather | solution.py:21
  21.9 119.6 %copy-start.1 = (bf16[1,1,197,768]{3,2,1,0:T(8,128)(2,1)S(1)}, bf16[1,1,197,768]{3,2,1,0:T(8,128)(2,1)}, u32[]{:S(2)}) copy-start(bf16[1,1,197,768]{3,2,1,0:T(8,128)(2,1)} %param.10) | copy-start | bytes 907780
  141.6 5.3 %copy-start.2 = (bf16[768,128]{1,0:T(8,128)(2,1)S(1)}, bf16[768,128]{1,0:T(8,128)(2,1)}, u32[]{:S(2)}) copy-start(bf16[768,128]{1,0:T(8,128)(2,1)} %param.14) | copy-start | bytes 589828
  147.3 2.2 copy-start.3
  149.9 72.8 %copy-start.4 = (f32[2,16,128]{2,1,0:T(8,128)S(1)}, f32[2,16,128]{2,1,0:T(8,128)}, u32[]{:S(2)}) copy-start(f32[2,16,128]{2,1,0:T(8,128)} %param.17) | copy-start | bytes 49156
  151.0 20.2 %all-to-all-start = ((f32[8,1,2,128,128]{4,3,2,1,0:T(8,128)}), f32[8,1,2,128,128]{4,3,2,1,0:T(8,128)S(1)}, u32[]{:S(2)}, u32[]{:S(2)}) async-start(f32[8,1,2,128,128]{4,3,2,1,0:T(8,128)} %broadcast_in_dim.10), calls=%async_computation | async-start | bytes 2097152 | tf_op jit(solution)/shard_map/all_to_all | solution.py:26
Sparse Core Ops, SparseCore 0:
  22.1 115.4 all-gather.4
